TPU v7x, 32 devices: a whole 2x2x4 slice. The times are simulated.
32 devices in a mesh: scan: 4 (over y, x), slab: 8 (over z, core).
Axes of the slice: x: 2, y: 2, z: 4, core: 2. Of those that a mesh axis runs over, the one named last changes fastest.
Arguments:
- solution: float32 [1536, 2048], P(('scan', 'slab')), parts along dimension 0, may hold values from -6 to 6
- direction: float32 [1536, 2048], P(('scan', 'slab')), parts along dimension 0, may hold values from -20 to 20
- gradient: float32 [1536, 2048], P(('scan', 'slab')), parts along dimension 0, may hold values from -40 to 40
- residual: float32 [512, 64, 896], P(('scan', 'slab')), parts along dimension 0, may hold values from -20 to 20
- tiles: bfloat16 [4, 2048, 896], replicated, may hold values from -0.125 to 0.125
- offsets: int32 [512], P(('scan', 'slab')), parts along dimension 0, may hold values from 1 to 320, as said below
Outputs:
- solution_next: float32 [1536, 2048], P(('scan', 'slab')), parts along dimension 0
- residual_next: float32 [512, 64, 896], P(('scan', 'slab')), parts along dimension 0
- gradient_next: float32 [1536, 2048], P(('scan', 'slab')), parts along dimension 0
- direction_next: float32 [1536, 2048], P(('scan', 'slab')), parts along dimension 0
There are 4 independent parts, one for each index of `scan`. A program takes and returns all parts, laid end to end along the dimension named above; an argument that names none is the same for every part. Nothing has to cross between parts.
Inputs may be any that keep to these rules, and one draw needn't show every extreme that they name: View v belongs to slab v // 16, whose planes are s * 48 to s * 48 + 47 for slab s; its window offsets[v] to offsets[v] + 63 meets that slab and lies within the slab before it, the slab itself and the slab after it; offsets are 1 or more.
All inputs are finite; a program needn't handle non-finite values.
Results may differ from a plain program's by a relative error of at most 0.0029.
Values may be sent and summed in bfloat16 or wider, within the bound.
A program may use at most 192 MiB of HBM per device.

v0:
```python
import functools

import jax
import jax.numpy as jnp
from jax import lax
from jax.experimental import pallas as pl
from jax.experimental.pallas import tpu as pltpu
from jax.sharding import PartitionSpec as P

CHUNK = 256
LANES = 128
VMEM_MIB = 38


def fold_lanes(row):
    total = row[:, :LANES]
    for start in range(LANES, row.shape[1], LANES):
        total = total + row[:, start : start + LANES]
    return total


def kernel(
    count,
    offsets_ref,
    direction_hbm,
    gradient_hbm,
    residual_hbm,
    tiles_hbm,
    residual_out,
    gradient_out,
    stats_out,
    direction_vm,
    gradient_vm,
    residual_vm,
    tiles_vm,
    nearby,
    projected,
    windows,
    hits,
    picks,
    half,
    summed,
    center,
    outgoing,
    incoming,
    stat_send,
    stat_recv,
    stats_vm,
    local_sems,
    tile_sems,
    halo_send,
    halo_recv,
    stat_send_sems,
    stat_recv_sems,
    back_send,
    back_recv,
):
    me = lax.axis_index("slab")
    planes, cells = direction_vm.shape
    views, rows, columns = residual_vm.shape
    angles = tiles_vm.shape[0]
    per_angle = views // angles
    near = 3 * planes
    chunks = cells // CHUNK
    has_low = me > 0
    has_high = me < count - 1

    load_direction = pltpu.make_async_copy(direction_hbm, direction_vm, local_sems.at[0])
    load_gradient = pltpu.make_async_copy(gradient_hbm, gradient_vm, local_sems.at[1])
    load_residual = pltpu.make_async_copy(residual_hbm, residual_vm, local_sems.at[2])

    def load_tile(a):
        return pltpu.make_async_copy(tiles_hbm.at[a], tiles_vm.at[a], tile_sems.at[a])

    load_direction.start()
    for a in range(angles):
        load_tile(a).start()
    load_gradient.start()
    load_residual.start()

    barrier = pltpu.get_barrier_semaphore()
    for d in range(1, count):
        pl.semaphore_signal(barrier, inc=1, device_id={"slab": lax.rem(me + d, count)})

    load_direction.wait()
    nearby[planes : 2 * planes, :] = direction_vm[...].astype(jnp.bfloat16)

    pad = jnp.zeros((planes, cells), jnp.bfloat16)

    @pl.when(jnp.logical_not(has_low))
    def _():
        nearby[:planes, :] = pad
        incoming[:, 1] = jnp.zeros((chunks, planes, CHUNK), jnp.float32)

    @pl.when(jnp.logical_not(has_high))
    def _():
        nearby[2 * planes :, :] = pad
        incoming[:, 0] = jnp.zeros((chunks, planes, CHUNK), jnp.float32)

    pl.semaphore_wait(barrier, count - 1)

    own = nearby.at[pl.ds(planes, planes)]
    to_low = pltpu.make_async_remote_copy(
        own, nearby.at[pl.ds(2 * planes, planes)], halo_send.at[0], halo_recv.at[0],
        device_id={"slab": lax.rem(me + count - 1, count)},
    )
    to_high = pltpu.make_async_remote_copy(
        own, nearby.at[pl.ds(0, planes)], halo_send.at[1], halo_recv.at[1],
        device_id={"slab": lax.rem(me + 1, count)},
    )

    @pl.when(has_low)
    def _():
        to_low.start()

    @pl.when(has_high)
    def _():
        to_high.start()

    plane_id = lax.broadcasted_iota(jnp.int32, (near, per_angle * rows), 0)
    row_id = lax.broadcasted_iota(jnp.int32, (near, per_angle * rows), 1)
    row_of = lax.broadcasted_iota(jnp.int32, (per_angle * rows, near), 0)
    plane_of = lax.broadcasted_iota(jnp.int32, (per_angle * rows, near), 1)
    shift = planes - me * planes
    for a in range(angles):
        base = jnp.zeros_like(row_id)
        for j in range(per_angle):
            first = offsets_ref[j * angles + a] + shift
            base = jnp.where(row_id >= j * rows, first - j * rows, base)
        hits[a] = jnp.where(plane_id == row_id + base, 1.0, 0.0).astype(jnp.bfloat16)
        base = jnp.zeros_like(row_of)
        for j in range(per_angle):
            first = offsets_ref[j * angles + a] + shift
            base = jnp.where(row_of >= j * rows, first - j * rows, base)
        picks[a] = jnp.where(plane_of == row_of + base, 1.0, 0.0).astype(jnp.bfloat16)

    @pl.when(has_low)
    def _():
        to_low.wait_send()
        to_high_recv = to_high
        to_high_recv.wait_recv()

    @pl.when(has_high)
    def _():
        to_high.wait_send()
        to_low.wait_recv()

    def forward(a, total):
        load_tile(a).wait()
        image = jnp.dot(nearby[...], tiles_vm[a], preferred_element_type=jnp.float32)
        upper = image.astype(jnp.bfloat16)
        projected[a, 0] = upper
        projected[a, 1] = (image - upper.astype(jnp.float32)).astype(jnp.bfloat16)
        covering = jnp.sum(hits[a].astype(jnp.float32), axis=1, keepdims=True)
        return total + jnp.sum(image * image * covering, axis=0, keepdims=True)

    image_part = lax.fori_loop(0, angles, forward, jnp.zeros((1, columns), jnp.float32))
    load_gradient.wait()
    grad_part = jnp.sum(gradient_vm[...] * gradient_vm[...], axis=0, keepdims=True)

    def exchange(index):
        copies = []
        for d in range(1, count):
            copies.append(
                pltpu.make_async_remote_copy(
                    stat_send.at[index], stat_recv.at[index, d],
                    stat_send_sems.at[index, d], stat_recv_sems.at[index, d],
                    device_id={"slab": lax.rem(me + d, count)},
                )
            )
        for copy in copies:
            copy.start()
        return copies

    def gather(index, copies):
        total = stat_send[index]
        for d, copy in enumerate(copies):
            copy.wait()
            total = total + stat_recv[index, d + 1]
        return total

    stat_send[0] = jnp.concatenate(
        [fold_lanes(grad_part), fold_lanes(image_part), jnp.zeros((6, LANES), jnp.float32)], axis=0
    )
    copies = exchange(0)

    def pick(a, carry):
        windows[a] = jnp.dot(picks[a], projected[a, 0], preferred_element_type=jnp.float32) + jnp.dot(
            picks[a], projected[a, 1], preferred_element_type=jnp.float32
        )
        return carry

    lax.fori_loop(0, angles, pick, 0)
    load_residual.wait()
    norms = gather(0, copies)
    grad_norm = jnp.sum(norms[0:1], axis=1, keepdims=True)
    image_norm = jnp.sum(norms[1:2], axis=1, keepdims=True)
    step_size = grad_norm / image_norm

    def update(v, carry):
        a = lax.rem(v, angles)
        j = lax.div(v, angles)
        image = windows[a, pl.ds(pl.multiple_of(j * rows, rows), rows), :]
        residual_next = residual_vm[v] - step_size * image
        residual_vm[v] = residual_next
        half[a, pl.ds(pl.multiple_of(j * rows, rows), rows), :] = residual_next.astype(jnp.bfloat16)
        return carry

    lax.fori_loop(0, views, update, 0)
    store_residual = pltpu.make_async_copy(residual_vm, residual_out, local_sems.at[3])
    store_residual.start()

    def gather_rows(a, carry):
        summed[a] = jnp.dot(hits[a], half[a], preferred_element_type=jnp.float32).astype(jnp.bfloat16)
        return carry

    lax.fori_loop(0, angles, gather_rows, 0)

    def back_copy(side, j):
        target = lax.rem(me + (count - 1 if side == 0 else 1), count)
        return pltpu.make_async_remote_copy(
            outgoing.at[j, side], incoming.at[j, side], back_send.at[side, j], back_recv.at[side, j],
            device_id={"slab": target},
        )

    def backward(j, carry):
        cut = pl.ds(pl.multiple_of(j * CHUNK, CHUNK), CHUNK)
        total = jnp.zeros((near, CHUNK), jnp.float32)
        for a in range(angles):
            total = total + lax.dot_general(
                summed[a], tiles_vm[a, cut, :], (((1,), (1,)), ((), ())),
                preferred_element_type=jnp.float32,
            )
        outgoing[j, 0] = total[:planes]
        outgoing[j, 1] = total[2 * planes :]
        center[j] = total[planes : 2 * planes]

        @pl.when(has_low)
        def _():
            back_copy(0, j).start()

        @pl.when(has_high)
        def _():
            back_copy(1, j).start()

        return carry

    lax.fori_loop(0, chunks, backward, 0)

    def combine(j, total):
        @pl.when(has_low)
        def _():
            back_copy(0, j).wait_send()
            back_copy(1, j).wait_recv()

        @pl.when(has_high)
        def _():
            back_copy(1, j).wait_send()
            back_copy(0, j).wait_recv()

        new = center[j] + incoming[j, 0] + incoming[j, 1]
        gradient_vm[:, pl.ds(pl.multiple_of(j * CHUNK, CHUNK), CHUNK)] = new
        return total + jnp.sum(new * new, axis=0, keepdims=True)

    new_part = lax.fori_loop(0, chunks, combine, jnp.zeros((1, CHUNK), jnp.float32))
    stat_send[1] = jnp.concatenate([fold_lanes(new_part), jnp.zeros((7, LANES), jnp.float32)], axis=0)
    copies = exchange(1)
    store_gradient = pltpu.make_async_copy(gradient_vm, gradient_out, local_sems.at[4])
    store_gradient.start()
    new_norm = jnp.sum(gather(1, copies)[0:1], axis=1, keepdims=True)
    stats_vm[...] = jnp.concatenate(
        [
            jnp.broadcast_to(step_size, (1, LANES)),
            jnp.broadcast_to(new_norm / grad_norm, (1, LANES)),
            jnp.zeros((6, LANES), jnp.float32),
        ],
        axis=0,
    )
    store_stats = pltpu.make_async_copy(stats_vm, stats_out, local_sems.at[5])
    store_stats.start()
    store_residual.wait()
    store_gradient.wait()
    store_stats.wait()


def finish(
    stats, solution_ref, direction_ref, gradient_ref, residual_ref,
    solution_out, residual_out, gradient_out, direction_out,
    solution_vm, direction_vm, gradient_vm, sems, residual_vm, residual_in, residual_sems,
):
    pieces = residual_ref.shape[0] // residual_vm.shape[1]
    span = residual_vm.shape[1]

    def part_in(p):
        return pltpu.make_async_copy(
            residual_ref.at[pl.ds(p * span, span)], residual_vm.at[p], residual_in.at[p]
        )

    def part_out(p):
        return pltpu.make_async_copy(
            residual_vm.at[p], residual_out.at[pl.ds(p * span, span)], residual_sems.at[p]
        )

    loads = [
        pltpu.make_async_copy(gradient_ref, gradient_vm, sems.at[0]),
        pltpu.make_async_copy(direction_ref, direction_vm, sems.at[1]),
        pltpu.make_async_copy(solution_ref, solution_vm, sems.at[2]),
    ]
    for p in range(pieces):
        part_in(p).start()
    for load in loads:
        load.start()
    for p in range(pieces):
        part_in(p).wait()
        part_out(p).start()
    for load in loads:
        load.wait()
    stores = [
        pltpu.make_async_copy(gradient_vm, gradient_out, sems.at[3]),
        pltpu.make_async_copy(direction_vm, direction_out, sems.at[4]),
        pltpu.make_async_copy(solution_vm, solution_out, sems.at[5]),
    ]
    stores[0].start()
    solution_vm[...] = solution_vm[...] + stats[0:1, 0:1] * direction_vm[...]
    stores[2].start()
    direction_vm[...] = gradient_vm[...] + stats[1:2, 0:1] * direction_vm[...]
    stores[1].start()
    for store in stores:
        store.wait()
    for p in range(pieces):
        part_out(p).wait()


def local(count, solution, direction, gradient, residual, tiles, offsets):
    planes, cells = solution.shape
    views, rows, columns = residual.shape
    angles = tiles.shape[0]
    per_angle = views // angles
    near = 3 * planes
    chunks = cells // CHUNK
    f32, bf16 = jnp.float32, jnp.bfloat16
    anywhere = pl.BlockSpec(memory_space=pl.ANY)
    residual_next, gradient_next, stats = pl.pallas_call(
        functools.partial(kernel, count),
        name="cgls_step",
        out_shape=(
            jax.ShapeDtypeStruct(residual.shape, f32),
            jax.ShapeDtypeStruct(gradient.shape, f32),
            jax.ShapeDtypeStruct((8, LANES), f32),
        ),
        in_specs=[pl.BlockSpec(memory_space=pltpu.SMEM)] + [anywhere] * 4,
        out_specs=(anywhere,) * 3,
        scratch_shapes=[
            pltpu.VMEM((planes, cells), f32),
            pltpu.VMEM((planes, cells), f32),
            pltpu.VMEM((views, rows, columns), f32),
            pltpu.VMEM((angles, cells, columns), bf16),
            pltpu.VMEM((near, cells), bf16),
            pltpu.VMEM((angles, 2, near, columns), bf16),
            pltpu.VMEM((angles, per_angle * rows, columns), f32),
            pltpu.VMEM((angles, near, per_angle * rows), bf16),
            pltpu.VMEM((angles, per_angle * rows, near), bf16),
            pltpu.VMEM((angles, per_angle * rows, columns), bf16),
            pltpu.VMEM((angles, near, columns), bf16),
            pltpu.VMEM((chunks, planes, CHUNK), f32),
            pltpu.VMEM((chunks, 2, planes, CHUNK), f32),
            pltpu.VMEM((chunks, 2, planes, CHUNK), f32),
            pltpu.VMEM((2, 8, LANES), f32),
            pltpu.VMEM((2, count, 8, LANES), f32),
            pltpu.VMEM((8, LANES), f32),
            pltpu.SemaphoreType.DMA((6,)),
            pltpu.SemaphoreType.DMA((angles,)),
            pltpu.SemaphoreType.DMA((2,)),
            pltpu.SemaphoreType.DMA((2,)),
            pltpu.SemaphoreType.DMA((2, count)),
            pltpu.SemaphoreType.DMA((2, count)),
            pltpu.SemaphoreType.DMA((2, chunks)),
            pltpu.SemaphoreType.DMA((2, chunks)),
        ],
        compiler_params=pltpu.CompilerParams(
            collective_id=0, has_side_effects=True, vmem_limit_bytes=VMEM_MIB * 1024 * 1024
        ),
    )(offsets, direction, gradient, residual, tiles)
    pieces = angles
    volume = jax.ShapeDtypeStruct(solution.shape, f32)
    return pl.pallas_call(
        finish,
        name="finish",
        out_shape=(volume, jax.ShapeDtypeStruct(residual.shape, f32), volume, volume),
        in_specs=[pl.BlockSpec(memory_space=pltpu.VMEM)] + [anywhere] * 4,
        out_specs=(anywhere,) * 4,
        scratch_shapes=[
            pltpu.VMEM((planes, cells), f32),
            pltpu.VMEM((planes, cells), f32),
            pltpu.VMEM((planes, cells), f32),
            pltpu.SemaphoreType.DMA((6,)),
            pltpu.VMEM((pieces, views // pieces, rows, columns), f32),
            pltpu.SemaphoreType.DMA((pieces,)),
            pltpu.SemaphoreType.DMA((pieces,)),
        ],
        compiler_params=pltpu.CompilerParams(vmem_limit_bytes=16 * 1024 * 1024),
    )(stats, solution, direction, gradient_next, residual_next)


def solution(mesh):
    placed = (
        P(("scan", "slab"), None),
        P(("scan", "slab"), None),
        P(("scan", "slab"), None),
        P(("scan", "slab"), None, None),
        P(),
        P(("scan", "slab")),
    )
    return jax.shard_map(
        functools.partial(local, mesh.shape["slab"]),
        mesh=mesh,
        in_specs=placed,
        out_specs=(
            P(("scan", "slab"), None),
            P(("scan", "slab"), None, None),
            P(("scan", "slab"), None),
            P(("scan", "slab"), None),
        ),
        check_vma=False,
    )
```

profile of v0, /device:TPU:0, one launch (start us, length us, event | category | flops | bytes accessed | tf_op | source)
XLA Modules:
  0.0 40.3 jit_solution(3580992983580587624)
XLA Ops:
  0.6 0.0 copy-start
  0.6 2.0 %copy-done = f32[16,64,896]{2,1,0:T(8,128)S(1)} copy-done((f32[16,64,896]{2,1,0:T(8,128)S(1)}, f32[16,64,896]{2,1,0:T(8,128)}, u32[]{:S(2)}) %copy-start) | copy-done | bytes 3670040
  2.7 0.0 copy-start.1
  2.7 1.0 %copy-done.1 = f32[48,2048]{1,0:T(8,128)S(1)} copy-done((f32[48,2048]{1,0:T(8,128)S(1)}, f32[48,2048]{1,0:T(8,128)}, u32[]{:S(2)}) %copy-start.1) | copy-done | bytes 393240
  3.7 0.0 copy-start.2
  3.7 1.0 %copy-done.2 = f32[48,2048]{1,0:T(8,128)S(1)} copy-done((f32[48,2048]{1,0:T(8,128)S(1)}, f32[48,2048]{1,0:T(8,128)}, u32[]{:S(2)}) %copy-start.2) | copy-done | bytes 393240
  4.7 0.0 copy-start.4
  4.7 0.7 %copy-done.4 = s32[16]{0:T(128)S(1)} copy-done((s32[16]{0:T(128)S(1)}, s32[16]{0:T(128)}, u32[]{:S(2)}) %copy-start.4) | copy-done | bytes 88
  5.3 0.0 copy-start.3
  5.3 31.1 %cgls_step.1 = (f32[16,64,896]{2,1,0:T(8,128)S(1)}, f32[48,2048]{1,0:T(8,128)S(1)}, f32[8,128]{1,0:T(8,128)S(1)}) custom-call(s32[16]{0:T(128)S(1)} %copy-done.4, f32[48,2048]{1,0:T(8,128)S(1)} %copy-done.1, f32[48,2048]{1,0:T(8,128)S(1)} %copy-done.2, f32[16,64,896]{2,1,0:T(8,128)S(1)} %copy-done, bf16[4,2048,896]{2,1,0:T(8,128)(2,1)} %tiles_hbm.1), custom_call_target="tpu_custom_call" | custom-call | tf_op jit(solution)/shard_map/cgls_step/pallas_call | solution.py:343
  36.5 0.0 copy-done.3
  36.5 3.8 %finish.1 = (f32[48,2048]{1,0:T(8,128)}, f32[16,64,896]{2,1,0:T(8,128)}, f32[48,2048]{1,0:T(8,128)}, f32[48,2048]{1,0:T(8,128)}) custom-call(f32[8,128]{1,0:T(8,128)S(1)} %get-tuple-element.7.stats, f32[48,2048]{1,0:T(8,128)S(1)} %copy-done.3, f32[48,2048]{1,0:T(8,128)S(1)} %copy-done.1, f32[48,2048]{1,0:T(8,128)S(1)} %get-tuple-element.8.gradient_ref, ...), custom_call_target="tpu_custom_call" | custom-call | tf_op jit(solution)/shard_map/finish/pallas_call | solution.py:386
Async XLA Ops:
  0.6 2.0 %copy-start = (f32[16,64,896]{2,1,0:T(8,128)S(1)}, f32[16,64,896]{2,1,0:T(8,128)}, u32[]{:S(2)}) copy-start(f32[16,64,896]{2,1,0:T(8,128)} %residual_hbm.1) | copy-start | bytes 11010052
  2.7 1.0 %copy-start.1 = (f32[48,2048]{1,0:T(8,128)S(1)}, f32[48,2048]{1,0:T(8,128)}, u32[]{:S(2)}) copy-start(f32[48,2048]{1,0:T(8,128)} %direction_ref.1) | copy-start | bytes 1179652
  3.7 1.0 %copy-start.2 = (f32[48,2048]{1,0:T(8,128)S(1)}, f32[48,2048]{1,0:T(8,128)}, u32[]{:S(2)}) copy-start(f32[48,2048]{1,0:T(8,128)} %gradient_hbm.1) | copy-start | bytes 1179652
  4.7 0.7 %copy-start.4 = (s32[16]{0:T(128)S(1)}, s32[16]{0:T(128)}, u32[]{:S(2)}) copy-start(s32[16]{0:T(128)} %offsets_ref.1) | copy-start | bytes 196
  5.3 31.1 %copy-start.3 = (f32[48,2048]{1,0:T(8,128)S(1)}, f32[48,2048]{1,0:T(8,128)}, u32[]{:S(2)}) copy-start(f32[48,2048]{1,0:T(8,128)} %solution_ref.1) | copy-start | bytes 1179652
where the time goes:
time: 40.5 us; the launch traced here: 40.3 us
  Pallas kernels  34.9 us (86%)
  local copies, waits for them, and re-layouts  4.68 us (12%)
  between operations  0.66 us (2%)
    pallas_call x1, Pallas kernels, local(): pl.pallas_call(functools.partial(kernel, count), name='cgls_step', out_sh...  31.1 us
    unnamed x10, local copies, waits for them, and re-layouts  4.68 us
    pallas_call x1, Pallas kernels, local(): pl.pallas_call(finish, name='finish', out_shape=(volume, jax.ShapeDtypeSt...  3.79 us

commit v1 on v0

v1 whole, which is shorter than its diff:
```python
import functools

import jax
import jax.numpy as jnp
from jax import lax
from jax.experimental import pallas as pl
from jax.experimental.pallas import tpu as pltpu
from jax.sharding import PartitionSpec as P

LANES = 128
STATS = 5
PROJECT_MIB = 30
FINISH_MIB = 8


def fold(value):
    total = value[:, :LANES]
    for start in range(LANES, value.shape[1], LANES):
        total = total + value[:, start : start + LANES]
    return jnp.sum(total, axis=0, keepdims=True)


def split(value):
    upper = value.astype(jnp.bfloat16)
    return upper, (value - upper.astype(jnp.float32)).astype(jnp.bfloat16)


def project(
    count,
    offsets_hbm,
    direction_hbm,
    gradient_hbm,
    residual_hbm,
    tiles_hbm,
    residual_vm,
    direction_vm,
    images,
    back_image,
    back_residual,
    stats_out,
    offsets_sm,
    gradient_vm,
    tiles_vm,
    own,
    halo,
    hits,
    covers,
    covers_in,
    sums_own,
    sums_out,
    sums_in,
    stacked,
    total,
    stat_send,
    stat_recv,
    load_sems,
    residual_sems,
    tile_sems,
    cover_send,
    cover_recv,
    sums_send,
    sums_recv,
    halo_send,
    halo_recv,
    stat_send_sems,
    stat_recv_sems,
):
    me = lax.axis_index("slab")
    planes, cells = direction_vm.shape
    angles, per_angle, rows, columns = residual_vm.shape
    near = 3 * planes
    f32, bf16 = jnp.float32, jnp.bfloat16
    has_low = me > 0
    has_high = me < count - 1
    low = {"slab": lax.rem(me + count - 1, count)}
    high = {"slab": lax.rem(me + 1, count)}

    load_offsets = pltpu.make_async_copy(offsets_hbm, offsets_sm, load_sems.at[0])
    load_direction = pltpu.make_async_copy(direction_hbm, direction_vm, load_sems.at[1])
    load_gradient = pltpu.make_async_copy(gradient_hbm, gradient_vm, load_sems.at[2])

    def load_residual(a):
        return pltpu.make_async_copy(residual_hbm.at[:, a], residual_vm.at[a], residual_sems.at[a])

    def load_tile(a):
        return pltpu.make_async_copy(tiles_hbm.at[a], tiles_vm.at[a], tile_sems.at[a])

    load_offsets.start()
    load_direction.start()
    for a in range(angles):
        load_residual(a).start()
    for a in range(angles):
        load_tile(a).start()
    load_gradient.start()

    barrier = pltpu.get_barrier_semaphore()
    for d in range(1, count):
        pl.semaphore_signal(barrier, inc=1, device_id={"slab": lax.rem(me + d, count)})

    @pl.when(jnp.logical_not(has_low))
    def _():
        halo[:planes, :] = jnp.zeros((planes, cells), bf16)
        covers_in[0] = jnp.zeros((planes, LANES), bf16)
        sums_in[:, 0] = jnp.zeros((angles, planes, columns), bf16)

    @pl.when(jnp.logical_not(has_high))
    def _():
        halo[planes:, :] = jnp.zeros((planes, cells), bf16)
        covers_in[1] = jnp.zeros((planes, LANES), bf16)
        sums_in[:, 1] = jnp.zeros((angles, planes, columns), bf16)

    load_offsets.wait()
    shift = planes - me * planes

    lane = lax.broadcasted_iota(jnp.int32, (near, LANES), 1)
    plane = lax.broadcasted_iota(jnp.int32, (near, LANES), 0)
    first = jnp.full((near, LANES), near, jnp.int32)
    for v in range(angles * per_angle):
        first = jnp.where(lane == v, offsets_sm[v] + shift, first)
    inside = jnp.logical_and(plane >= first, plane < first + rows)
    covers[...] = jnp.where(inside, 1.0, 0.0).astype(bf16)

    plane_id = lax.broadcasted_iota(jnp.int32, (near, per_angle * rows), 0)
    row_id = lax.broadcasted_iota(jnp.int32, (near, per_angle * rows), 1)
    for a in range(angles):
        base = jnp.zeros_like(row_id)
        for j in range(per_angle):
            base = jnp.where(row_id >= j * rows, offsets_sm[j * angles + a] + shift - j * rows, base)
        hits[a] = jnp.where(plane_id == row_id + base, 1.0, 0.0).astype(bf16)

    load_direction.wait()
    own[...] = direction_vm[...].astype(bf16)

    def cover_copy(side):
        source = covers.at[pl.ds(0 if side == 0 else 2 * planes, planes)]
        return pltpu.make_async_remote_copy(
            source, covers_in.at[1 - side], cover_send.at[side], cover_recv.at[1 - side],
            device_id=low if side == 0 else high,
        )

    def sums_copy(side, a):
        return pltpu.make_async_remote_copy(
            sums_out.at[a, side], sums_in.at[a, 1 - side], sums_send.at[side, a], sums_recv.at[1 - side, a],
            device_id=low if side == 0 else high,
        )

    def halo_copy(side):
        return pltpu.make_async_remote_copy(
            own, halo.at[pl.ds((1 - side) * planes, planes)], halo_send.at[side], halo_recv.at[1 - side],
            device_id=low if side == 0 else high,
        )

    pl.semaphore_wait(barrier, count - 1)

    @pl.when(has_low)
    def _():
        cover_copy(0).start()

    @pl.when(has_high)
    def _():
        cover_copy(1).start()

    def gather_rows(a, carry):
        load_residual(a).wait()
        upper, lower = split(residual_vm[a].reshape(per_angle * rows, columns))
        sums = jnp.dot(hits[a], upper, preferred_element_type=f32) + jnp.dot(
            hits[a], lower, preferred_element_type=f32
        )
        sums_own[a] = sums[planes : 2 * planes]
        sums_out[a, 0] = sums[:planes].astype(bf16)
        sums_out[a, 1] = sums[2 * planes :].astype(bf16)

        @pl.when(has_low)
        def _():
            sums_copy(0, a).start()

        @pl.when(has_high)
        def _():
            sums_copy(1, a).start()

        return carry

    lax.fori_loop(0, angles, gather_rows, 0)

    @pl.when(has_low)
    def _():
        halo_copy(0).start()
        cover_copy(0).wait_send()
        cover_copy(1).wait_recv()

    @pl.when(has_high)
    def _():
        halo_copy(1).start()
        cover_copy(1).wait_send()
        cover_copy(0).wait_recv()

    covered = covers[planes : 2 * planes].astype(f32) + covers_in[0].astype(f32) + covers_in[1].astype(f32)
    covered = covered.astype(bf16)
    view_of = lax.broadcasted_iota(jnp.int32, (LANES, LANES), 0)

    def forward(a, image_part):
        chosen = jnp.where(lax.rem(view_of, angles) == a, 1.0, 0.0).astype(bf16)
        times = jnp.dot(covered, chosen, preferred_element_type=f32)
        load_tile(a).wait()
        image = jnp.dot(own[...], tiles_vm[a], preferred_element_type=f32)
        for l in range(columns // LANES):
            cut = slice(l * LANES, (l + 1) * LANES)
            piece = image[:, cut]
            weighted = times * piece
            images[a, l, planes : 2 * planes] = piece
            stacked[a, :planes, cut] = weighted.astype(bf16)
            image_part = image_part + jnp.sum(weighted * piece, axis=0, keepdims=True)
        return image_part

    image_part = lax.fori_loop(0, angles, forward, jnp.zeros((1, LANES), f32))

    def backward(a, carry):
        @pl.when(has_low)
        def _():
            sums_copy(1, a).wait_recv()

        @pl.when(has_high)
        def _():
            sums_copy(0, a).wait_recv()

        sums = sums_own[a] + sums_in[a, 0].astype(f32) + sums_in[a, 1].astype(f32)
        upper, lower = split(sums)
        stacked[a, planes : 2 * planes] = upper
        stacked[a, 2 * planes :] = lower
        part = lax.dot_general(
            stacked[a], tiles_vm[a], (((1,), (1,)), ((), ())), preferred_element_type=f32
        )

        @pl.when(a == 0)
        def _():
            total[...] = part

        @pl.when(a > 0)
        def _():
            total[...] = total[...] + part

        return carry

    lax.fori_loop(0, angles, backward, 0)

    from_image = total[:planes]
    from_residual = total[planes : 2 * planes] + total[2 * planes :]
    back_image[...] = from_image
    back_residual[...] = from_residual
    load_gradient.wait()
    gradient = gradient_vm[...]
    stat_send[...] = jnp.concatenate(
        [
            fold(gradient * gradient),
            image_part,
            fold(from_residual * from_residual),
            fold(from_residual * from_image),
            fold(from_image * from_image),
            jnp.zeros((8 - STATS, LANES), f32),
        ],
        axis=0,
    )
    copies = []
    for d in range(1, count):
        copies.append(
            pltpu.make_async_remote_copy(
                stat_send, stat_recv.at[d], stat_send_sems.at[d], stat_recv_sems.at[d],
                device_id={"slab": lax.rem(me + d, count)},
            )
        )
    for copy in copies:
        copy.start()

    @pl.when(has_low)
    def _():
        halo_copy(0).wait_send()
        halo_copy(1).wait_recv()

    @pl.when(has_high)
    def _():
        halo_copy(1).wait_send()
        halo_copy(0).wait_recv()

    def forward_halo(a, carry):
        image = jnp.dot(halo[...], tiles_vm[a], preferred_element_type=f32)
        for l in range(columns // LANES):
            cut = slice(l * LANES, (l + 1) * LANES)
            images[a, l, :planes] = image[:planes, cut]
            images[a, l, 2 * planes :] = image[planes:, cut]
        return carry

    lax.fori_loop(0, angles, forward_halo, 0)

    @pl.when(has_low)
    def _():
        for a in range(angles):
            sums_copy(0, a).wait_send()

    @pl.when(has_high)
    def _():
        for a in range(angles):
            sums_copy(1, a).wait_send()

    sums = stat_send[...]
    for d, copy in enumerate(copies):
        copy.wait()
        sums = sums + stat_recv[d + 1]
    norms = jnp.sum(sums, axis=1, keepdims=True)
    grad_norm, image_norm = norms[0:1], norms[1:2]
    step_size = grad_norm / image_norm
    new_norm = norms[2:3] - 2.0 * step_size * norms[3:4] + step_size * step_size * norms[4:5]
    stats_out[...] = jnp.concatenate(
        [
            jnp.broadcast_to(step_size, (1, LANES)),
            jnp.broadcast_to(new_norm / grad_norm, (1, LANES)),
            jnp.zeros((6, LANES), f32),
        ],
        axis=0,
    )


def finish(
    offsets_ref, stats, solution_ref, direction_ref, back_image, back_residual, images, residual_ref,
    solution_out, residual_out, gradient_out, direction_out,
    solution_vm, gradient_vm, direction_vm, residual_vm, sems, residual_sems,
):
    me = lax.axis_index("slab")
    planes = direction_ref.shape[0]
    angles, per_angle, rows, columns = residual_ref.shape
    step_size = stats[0:1, 0:1]
    scale = stats[1:2, 0:1]
    stores = [
        pltpu.make_async_copy(gradient_vm, gradient_out, sems.at[0]),
        pltpu.make_async_copy(direction_vm, direction_out, sems.at[1]),
        pltpu.make_async_copy(solution_vm, solution_out, sems.at[2]),
    ]
    gradient = back_residual[...] - step_size * back_image[...]
    gradient_vm[...] = gradient
    stores[0].start()
    direction_vm[...] = gradient + scale * direction_ref[...]
    stores[1].start()
    solution_vm[...] = solution_ref[...] + step_size * direction_ref[...]
    stores[2].start()

    def store_view(j, a):
        return pltpu.make_async_copy(residual_vm.at[j, a], residual_out.at[j, a], residual_sems.at[j, a])

    shift = planes - me * planes
    for j in range(per_angle):
        for a in range(angles):
            first = offsets_ref[j * angles + a] + shift
            for l in range(columns // LANES):
                cut = slice(l * LANES, (l + 1) * LANES)
                window = images[a, l, pl.ds(first, rows), :]
                residual_vm[j, a, :, cut] = residual_ref[a, j, :, cut] - step_size * window
            store_view(j, a).start()
    for store in stores:
        store.wait()
    for j in range(per_angle):
        for a in range(angles):
            store_view(j, a).wait()


def local(count, solution, direction, gradient, residual, tiles, offsets):
    planes, cells = solution.shape
    views, rows, columns = residual.shape
    angles = tiles.shape[0]
    per_angle = views // angles
    near = 3 * planes
    f32, bf16 = jnp.float32, jnp.bfloat16
    hbm = pl.BlockSpec(memory_space=pltpu.HBM)
    vmem = pl.BlockSpec(memory_space=pltpu.VMEM)
    smem = pl.BlockSpec(memory_space=pltpu.SMEM)
    dma = pltpu.SemaphoreType.DMA
    by_angle = residual.reshape(per_angle, angles, rows, columns)
    volume = jax.ShapeDtypeStruct((planes, cells), f32)
    remote = [pltpu.with_memory_space_constraint(x, pltpu.HBM) for x in (offsets, direction, gradient, by_angle, tiles)]
    residual_in, direction_in, images, back_image, back_residual, stats = pl.pallas_call(
        functools.partial(project, count),
        name="project",
        out_shape=(
            jax.ShapeDtypeStruct((angles, per_angle, rows, columns), f32),
            volume,
            jax.ShapeDtypeStruct((angles, columns // LANES, near, LANES), f32),
            volume,
            volume,
            jax.ShapeDtypeStruct((8, LANES), f32),
        ),
        in_specs=[hbm] * 5,
        out_specs=(vmem,) * 6,
        scratch_shapes=[
            pltpu.SMEM((views,), jnp.int32),
            pltpu.VMEM((planes, cells), f32),
            pltpu.VMEM((angles, cells, columns), bf16),
            pltpu.VMEM((planes, cells), bf16),
            pltpu.VMEM((2 * planes, cells), bf16),
            pltpu.VMEM((angles, near, per_angle * rows), bf16),
            pltpu.VMEM((near, LANES), bf16),
            pltpu.VMEM((2, planes, LANES), bf16),
            pltpu.VMEM((angles, planes, columns), f32),
            pltpu.VMEM((angles, 2, planes, columns), bf16),
            pltpu.VMEM((angles, 2, planes, columns), bf16),
            pltpu.VMEM((angles, near, columns), bf16),
            pltpu.VMEM((near, cells), f32),
            pltpu.VMEM((8, LANES), f32),
            pltpu.VMEM((count, 8, LANES), f32),
            dma((3,)),
            dma((angles,)),
            dma((angles,)),
            dma((2,)),
            dma((2,)),
            dma((2, angles)),
            dma((2, angles)),
            dma((2,)),
            dma((2,)),
            dma((count,)),
            dma((count,)),
        ],
        compiler_params=pltpu.CompilerParams(
            collective_id=0, has_side_effects=True, vmem_limit_bytes=PROJECT_MIB * 1024 * 1024
        ),
    )(*remote)
    results = pl.pallas_call(
        finish,
        name="finish",
        out_shape=(volume, jax.ShapeDtypeStruct((per_angle, angles, rows, columns), f32), volume, volume),
        in_specs=[smem] + [vmem] * 7,
        out_specs=(hbm,) * 4,
        scratch_shapes=[
            pltpu.VMEM((planes, cells), f32),
            pltpu.VMEM((planes, cells), f32),
            pltpu.VMEM((planes, cells), f32),
            pltpu.VMEM((per_angle, angles, rows, columns), f32),
            dma((3,)),
            dma((per_angle, angles)),
        ],
        compiler_params=pltpu.CompilerParams(vmem_limit_bytes=FINISH_MIB * 1024 * 1024),
    )(offsets, stats, solution, direction_in, back_image, back_residual, images, residual_in)
    return results[0], results[1].reshape(residual.shape), results[2], results[3]


def solution(mesh):
    placed = (
        P(("scan", "slab"), None),
        P(("scan", "slab"), None),
        P(("scan", "slab"), None),
        P(("scan", "slab"), None, None),
        P(),
        P(("scan", "slab")),
    )
    return jax.shard_map(
        functools.partial(local, mesh.shape["slab"]),
        mesh=mesh,
        in_specs=placed,
        out_specs=(
            P(("scan", "slab"), None),
            P(("scan", "slab"), None, None),
            P(("scan", "slab"), None),
            P(("scan", "slab"), None),
        ),
        check_vma=False,
    )
```

time: 40.5 us -> 26.3 us (0.65)
  Pallas kernels: 34.9 us -> 25.4 us
  local copies, waits for them, and re-layouts: 4.68 us -> 0.01 us
    pallas_call x1, Pallas kernels: 31.1 us -> 22.5 us  [local(): pl.pallas_call(functools.partial(project, count), name='project', out_sha...]
    unnamed x10 -> x4, local copies, waits for them, and re-layouts: 4.68 us -> 0.01 us
    pallas_call x1, Pallas kernels: 3.79 us -> 2.96 us  [local(): pl.pallas_call(finish, name='finish', out_shape=(volume, jax.ShapeDtypeSt...]
where the time goes in v1:
time: 26.3 us; the launch traced here: 26.1 us
  Pallas kernels  25.4 us (97%)
  between operations  0.67 us (3%)
    pallas_call x1, Pallas kernels, local(): pl.pallas_call(functools.partial(project, count), name='project', out_sha...  22.5 us
    pallas_call x1, Pallas kernels, local(): pl.pallas_call(finish, name='finish', out_shape=(volume, jax.ShapeDtypeSt...  2.96 us

profile of v1, /device:TPU:0, one launch (start us, length us, event | category | flops | bytes accessed | tf_op | source)
XLA Modules:
  0.0 26.1 jit_solution(13104264737762585653)
XLA Ops:
  0.6 0.0 copy-start
  0.6 0.0 copy-start.1
  0.7 22.5 %project.1 = (f32[4,4,64,896]{3,2,1,0:T(8,128)S(1)}, f32[48,2048]{1,0:T(8,128)S(1)}, f32[4,7,144,128]{3,2,1,0:T(8,128)S(1)}, f32[48,2048]{1,0:T(8,128)S(1)}, f32...) custom-call(s32[16]{0:T(128)} %offsets_ref.1, f32[48,2048]{1,0:T(8,128)} %direction_hbm.1, f32[48,2048]{1,0:T(8,128)} %gradient_hbm.1, ...), custom_call_target="tpu_custom_call" | custom-call | tf_op jit(solution)/shard_map/project/pallas_call | solution.py:378
  23.1 0.0 copy-done
  23.2 0.0 copy-done.1
  23.2 3.0 %finish.1 = (f32[48,2048]{1,0:T(8,128)}, f32[4,4,64,896]{3,2,1,0:T(8,128)}, f32[48,2048]{1,0:T(8,128)}, f32[48,2048]{1,0:T(8,128)}) custom-call(s32[16]{0:T(128)S(1)} %copy-done.1, f32[8,128]{1,0:T(8,128)S(1)} %get-tuple-element.14.stats, f32[48,2048]{1,0:T(8,128)S(1)} %copy-done, f32[48,2048]{1,0:T(8,128)S(1)} %get-tuple-element.15.direction_ref, ...), custom_call_target="tpu_custom_call" | custom-call | tf_op jit(solution)/shard_map/finish/pallas_call | solution.py:423
Async XLA Ops:
  0.6 22.5 %copy-start = (f32[48,2048]{1,0:T(8,128)S(1)}, f32[48,2048]{1,0:T(8,128)}, u32[]{:S(2)}) copy-start(f32[48,2048]{1,0:T(8,128)} %solution_ref.1) | copy-start | bytes 1179652
  0.6 22.5 %copy-start.1 = (s32[16]{0:T(128)S(1)}, s32[16]{0:T(128)}, u32[]{:S(2)}) copy-start(s32[16]{0:T(128)} %offsets_ref.1) | copy-start | bytes 196

commit v2 on v1

--- a/solution.py
+++ b/solution.py
@@ -13,16 +13,18 @@
 FINISH_MIB = 8
 
 
-def fold(value):
-    total = value[:, :LANES]
-    for start in range(LANES, value.shape[1], LANES):
-        total = total + value[:, start : start + LANES]
-    return jnp.sum(total, axis=0, keepdims=True)
-
-
 def split(value):
     upper = value.astype(jnp.bfloat16)
     return upper, (value - upper.astype(jnp.float32)).astype(jnp.bfloat16)
+
+
+def fold_tile(value):
+    total = None
+    for r in range(0, value.shape[0], 8):
+        for c in range(0, value.shape[1], LANES):
+            tile = value[r : r + 8, c : c + LANES]
+            total = tile if total is None else total + tile
+    return total
 
 
 def project(
@@ -50,7 +52,7 @@
     sums_out,
     sums_in,
     stacked,
-    total,
+    partial,
     stat_send,
     stat_recv,
     load_sems,
@@ -65,6 +67,7 @@
     stat_send_sems,
     stat_recv_sems,
 ):
+    scope = jax.named_scope
     me = lax.axis_index("slab")
     planes, cells = direction_vm.shape
     angles, per_angle, rows, columns = residual_vm.shape
@@ -86,12 +89,12 @@
         return pltpu.make_async_copy(tiles_hbm.at[a], tiles_vm.at[a], tile_sems.at[a])
 
     load_offsets.start()
+    for a in range(angles):
+        load_residual(a).start()
     load_direction.start()
     for a in range(angles):
-        load_residual(a).start()
-    for a in range(angles):
-        load_tile(a).start()
-    load_gradient.start()
+        load_tile(a).start(priority=1)
+    load_gradient.start(priority=1)
 
     barrier = pltpu.get_barrier_semaphore()
     for d in range(1, count):
@@ -109,7 +112,8 @@
         covers_in[1] = jnp.zeros((planes, LANES), bf16)
         sums_in[:, 1] = jnp.zeros((angles, planes, columns), bf16)
 
-    load_offsets.wait()
+    with scope("w_off"):
+        load_offsets.wait()
     shift = planes - me * planes
 
     lane = lax.broadcasted_iota(jnp.int32, (near, LANES), 1)
@@ -128,9 +132,6 @@
             base = jnp.where(row_id >= j * rows, offsets_sm[j * angles + a] + shift - j * rows, base)
         hits[a] = jnp.where(plane_id == row_id + base, 1.0, 0.0).astype(bf16)
 
-    load_direction.wait()
-    own[...] = direction_vm[...].astype(bf16)
-
     def cover_copy(side):
         source = covers.at[pl.ds(0 if side == 0 else 2 * planes, planes)]
         return pltpu.make_async_remote_copy(
@@ -150,18 +151,9 @@
             device_id=low if side == 0 else high,
         )
 
-    pl.semaphore_wait(barrier, count - 1)
-
-    @pl.when(has_low)
-    def _():
-        cover_copy(0).start()
-
-    @pl.when(has_high)
-    def _():
-        cover_copy(1).start()
-
-    def gather_rows(a, carry):
-        load_residual(a).wait()
+    for a in range(angles):
+        with scope("w_res"):
+            load_residual(a).wait()
         upper, lower = split(residual_vm[a].reshape(per_angle * rows, columns))
         sums = jnp.dot(hits[a], upper, preferred_element_type=f32) + jnp.dot(
             hits[a], lower, preferred_element_type=f32
@@ -169,95 +161,114 @@
         sums_own[a] = sums[planes : 2 * planes]
         sums_out[a, 0] = sums[:planes].astype(bf16)
         sums_out[a, 1] = sums[2 * planes :].astype(bf16)
+        if a == 0:
+            with scope("w_bar"):
+                pl.semaphore_wait(barrier, count - 1)
 
         @pl.when(has_low)
         def _():
+            if a == 0:
+                cover_copy(0).start()
             sums_copy(0, a).start()
 
         @pl.when(has_high)
         def _():
+            if a == 0:
+                cover_copy(1).start()
             sums_copy(1, a).start()
 
-        return carry
-
-    lax.fori_loop(0, angles, gather_rows, 0)
+    with scope("w_dir"):
+        load_direction.wait()
+    own[...] = direction_vm[...].astype(bf16)
 
     @pl.when(has_low)
     def _():
         halo_copy(0).start()
-        cover_copy(0).wait_send()
-        cover_copy(1).wait_recv()
 
     @pl.when(has_high)
     def _():
         halo_copy(1).start()
-        cover_copy(1).wait_send()
-        cover_copy(0).wait_recv()
-
-    covered = covers[planes : 2 * planes].astype(f32) + covers_in[0].astype(f32) + covers_in[1].astype(f32)
-    covered = covered.astype(bf16)
-    view_of = lax.broadcasted_iota(jnp.int32, (LANES, LANES), 0)
-
-    def forward(a, image_part):
-        chosen = jnp.where(lax.rem(view_of, angles) == a, 1.0, 0.0).astype(bf16)
-        times = jnp.dot(covered, chosen, preferred_element_type=f32)
-        load_tile(a).wait()
+
+    view_of = lax.broadcasted_iota(jnp.int32, (LANES, angles * LANES), 0)
+    lane_of = lax.broadcasted_iota(jnp.int32, (LANES, angles * LANES), 1)
+    chosen = jnp.where(lax.rem(view_of, angles) == lane_of // LANES, 1.0, 0.0).astype(bf16)
+    image_sums = jnp.zeros((8, LANES), f32)
+    product_sums = [jnp.zeros((8, LANES), f32)] * 3
+    times = None
+
+    def backward(first_angle, last_angle):
+        chunk = 2 * LANES
+        for p in range(0, cells, chunk):
+            part = None
+            for a in range(first_angle, last_angle):
+                product = lax.dot_general(
+                    tiles_vm[a, p : p + chunk], stacked[a], (((1,), (1,)), ((), ())), preferred_element_type=f32
+                )
+                part = product if part is None else part + product
+            if first_angle > 0:
+                part = part + partial[p : p + chunk]
+            if last_angle < angles:
+                partial[p : p + chunk] = part
+                continue
+            turned = part.T
+            from_image, from_residual = turned[:planes], turned[planes:]
+            back_image[:, p : p + chunk] = from_image
+            back_residual[:, p : p + chunk] = from_residual
+            product_sums[0] = product_sums[0] + fold_tile(from_residual * from_residual)
+            product_sums[1] = product_sums[1] + fold_tile(from_residual * from_image)
+            product_sums[2] = product_sums[2] + fold_tile(from_image * from_image)
+
+    half = angles // 2
+    for a in range(angles):
+        with scope("w_tile"):
+            load_tile(a).wait()
+        if a == 0:
+            with scope("w_cov"):
+                @pl.when(has_low)
+                def _():
+                    cover_copy(0).wait_send()
+                    cover_copy(1).wait_recv()
+
+                @pl.when(has_high)
+                def _():
+                    cover_copy(1).wait_send()
+                    cover_copy(0).wait_recv()
+
+            covered = covers[planes : 2 * planes].astype(f32) + covers_in[0].astype(f32) + covers_in[1].astype(f32)
+            times = jnp.dot(covered.astype(bf16), chosen, preferred_element_type=f32)
         image = jnp.dot(own[...], tiles_vm[a], preferred_element_type=f32)
         for l in range(columns // LANES):
             cut = slice(l * LANES, (l + 1) * LANES)
             piece = image[:, cut]
-            weighted = times * piece
+            weighted = times[:, a * LANES : (a + 1) * LANES] * piece
             images[a, l, planes : 2 * planes] = piece
             stacked[a, :planes, cut] = weighted.astype(bf16)
-            image_part = image_part + jnp.sum(weighted * piece, axis=0, keepdims=True)
-        return image_part
-
-    image_part = lax.fori_loop(0, angles, forward, jnp.zeros((1, LANES), f32))
-
-    def backward(a, carry):
-        @pl.when(has_low)
-        def _():
-            sums_copy(1, a).wait_recv()
-
-        @pl.when(has_high)
-        def _():
-            sums_copy(0, a).wait_recv()
-
-        sums = sums_own[a] + sums_in[a, 0].astype(f32) + sums_in[a, 1].astype(f32)
-        upper, lower = split(sums)
-        stacked[a, planes : 2 * planes] = upper
-        stacked[a, 2 * planes :] = lower
-        part = lax.dot_general(
-            stacked[a], tiles_vm[a], (((1,), (1,)), ((), ())), preferred_element_type=f32
-        )
-
-        @pl.when(a == 0)
-        def _():
-            total[...] = part
-
-        @pl.when(a > 0)
-        def _():
-            total[...] = total[...] + part
-
-        return carry
-
-    lax.fori_loop(0, angles, backward, 0)
-
-    from_image = total[:planes]
-    from_residual = total[planes : 2 * planes] + total[2 * planes :]
-    back_image[...] = from_image
-    back_residual[...] = from_residual
-    load_gradient.wait()
-    gradient = gradient_vm[...]
+            image_sums = image_sums + fold_tile(weighted * piece)
+        ready = range(0, half) if a == half else range(half, angles) if a == angles - 1 else ()
+        if not ready:
+            continue
+        if a == angles - 1:
+            with scope("w_grad"):
+                load_gradient.wait()
+            gradient_sums = fold_tile(gradient_vm[...] * gradient_vm[...])
+        for b in ready:
+            with scope("w_sums"):
+                @pl.when(has_low)
+                def _():
+                    sums_copy(1, b).wait_recv()
+
+                @pl.when(has_high)
+                def _():
+                    sums_copy(0, b).wait_recv()
+
+            sums = sums_own[b] + sums_in[b, 0].astype(f32) + sums_in[b, 1].astype(f32)
+            stacked[b, planes:] = sums.astype(bf16)
+        with scope("bwd"):
+            backward(ready[0], ready[-1] + 1)
+
     stat_send[...] = jnp.concatenate(
-        [
-            fold(gradient * gradient),
-            image_part,
-            fold(from_residual * from_residual),
-            fold(from_residual * from_image),
-            fold(from_image * from_image),
-            jnp.zeros((8 - STATS, LANES), f32),
-        ],
+        [jnp.sum(x, axis=0, keepdims=True) for x in [gradient_sums, image_sums] + product_sums]
+        + [jnp.zeros((8 - STATS, LANES), f32)],
         axis=0,
     )
     copies = []
@@ -271,25 +282,24 @@
     for copy in copies:
         copy.start()
 
-    @pl.when(has_low)
-    def _():
-        halo_copy(0).wait_send()
-        halo_copy(1).wait_recv()
-
-    @pl.when(has_high)
-    def _():
-        halo_copy(1).wait_send()
-        halo_copy(0).wait_recv()
-
-    def forward_halo(a, carry):
-        image = jnp.dot(halo[...], tiles_vm[a], preferred_element_type=f32)
-        for l in range(columns // LANES):
-            cut = slice(l * LANES, (l + 1) * LANES)
-            images[a, l, :planes] = image[:planes, cut]
-            images[a, l, 2 * planes :] = image[planes:, cut]
-        return carry
-
-    lax.fori_loop(0, angles, forward_halo, 0)
+    with scope("w_halo"):
+        @pl.when(has_low)
+        def _():
+            halo_copy(0).wait_send()
+            halo_copy(1).wait_recv()
+
+        @pl.when(has_high)
+        def _():
+            halo_copy(1).wait_send()
+            halo_copy(0).wait_recv()
+
+    with scope("fwdhalo"):
+        for a in range(angles):
+            image = jnp.dot(halo[...], tiles_vm[a], preferred_element_type=f32)
+            for l in range(columns // LANES):
+                cut = slice(l * LANES, (l + 1) * LANES)
+                images[a, l, :planes] = image[:planes, cut]
+                images[a, l, 2 * planes :] = image[planes:, cut]
 
     @pl.when(has_low)
     def _():
@@ -301,22 +311,25 @@
         for a in range(angles):
             sums_copy(1, a).wait_send()
 
-    sums = stat_send[...]
-    for d, copy in enumerate(copies):
-        copy.wait()
-        sums = sums + stat_recv[d + 1]
-    norms = jnp.sum(sums, axis=1, keepdims=True)
-    grad_norm, image_norm = norms[0:1], norms[1:2]
-    step_size = grad_norm / image_norm
-    new_norm = norms[2:3] - 2.0 * step_size * norms[3:4] + step_size * step_size * norms[4:5]
-    stats_out[...] = jnp.concatenate(
-        [
-            jnp.broadcast_to(step_size, (1, LANES)),
-            jnp.broadcast_to(new_norm / grad_norm, (1, LANES)),
-            jnp.zeros((6, LANES), f32),
-        ],
-        axis=0,
-    )
+    with scope("w_stat"):
+        for copy in copies:
+            copy.wait()
+    with scope("stat"):
+        sums = stat_send[...]
+        for d in range(1, count):
+            sums = sums + stat_recv[d]
+        norms = jnp.sum(sums, axis=1, keepdims=True)
+        grad_norm, image_norm = norms[0:1], norms[1:2]
+        step_size = grad_norm / image_norm
+        new_norm = norms[2:3] - 2.0 * step_size * norms[3:4] + step_size * step_size * norms[4:5]
+        stats_out[...] = jnp.concatenate(
+            [
+                jnp.broadcast_to(step_size, (1, LANES)),
+                jnp.broadcast_to(new_norm / grad_norm, (1, LANES)),
+                jnp.zeros((6, LANES), f32),
+            ],
+            axis=0,
+        )
 
 
 def finish(
@@ -400,8 +413,8 @@
             pltpu.VMEM((angles, planes, columns), f32),
             pltpu.VMEM((angles, 2, planes, columns), bf16),
             pltpu.VMEM((angles, 2, planes, columns), bf16),
-            pltpu.VMEM((angles, near, columns), bf16),
-            pltpu.VMEM((near, cells), f32),
+            pltpu.VMEM((angles, 2 * planes, columns), bf16),
+            pltpu.VMEM((cells, 2 * planes), f32),
             pltpu.VMEM((8, LANES), f32),
             pltpu.VMEM((count, 8, LANES), f32),
             dma((3,)),

time: 26.3 us -> 22.5 us (0.86)
  Pallas kernels: 25.4 us -> 21.7 us
    pallas_call x1, Pallas kernels: 22.5 us -> 18.7 us  [local(): pl.pallas_call(functools.partial(project, count), name='project', out_sha...]
where the time goes in v2:
time: 22.5 us; the launch traced here: 22.3 us
  Pallas kernels  21.7 us (96%)
  between operations  0.67 us (3%)
    pallas_call x1, Pallas kernels, local(): pl.pallas_call(functools.partial(project, count), name='project', out_sha...  18.7 us
    pallas_call x1, Pallas kernels, local(): pl.pallas_call(finish, name='finish', out_shape=(volume, jax.ShapeDtypeSt...  2.96 us

profile of v2, /device:TPU:0, one launch (start us, length us, event | category | flops | bytes accessed | tf_op | source)
XLA Modules:
  0.0 22.3 jit_solution(17354527498587342275)
XLA Ops:
  0.6 0.0 copy-start
  0.6 0.0 copy-start.1
  0.7 18.7 %project.1 = (f32[4,4,64,896]{3,2,1,0:T(8,128)S(1)}, f32[48,2048]{1,0:T(8,128)S(1)}, f32[4,7,144,128]{3,2,1,0:T(8,128)S(1)}, f32[48,2048]{1,0:T(8,128)S(1)}, f32...) custom-call(s32[16]{0:T(128)} %offsets_ref.1, f32[48,2048]{1,0:T(8,128)} %direction_hbm.1, f32[48,2048]{1,0:T(8,128)} %gradient_hbm.1, ...), custom_call_target="tpu_custom_call" | custom-call | tf_op jit(solution)/shard_map/project/pallas_call | solution.py:391
  19.4 0.0 copy-done
  19.4 0.0 copy-done.1
  19.4 3.0 %finish.1 = (f32[48,2048]{1,0:T(8,128)}, f32[4,4,64,896]{3,2,1,0:T(8,128)}, f32[48,2048]{1,0:T(8,128)}, f32[48,2048]{1,0:T(8,128)}) custom-call(s32[16]{0:T(128)S(1)} %copy-done.1, f32[8,128]{1,0:T(8,128)S(1)} %get-tuple-element.14.stats, f32[48,2048]{1,0:T(8,128)S(1)} %copy-done, f32[48,2048]{1,0:T(8,128)S(1)} %get-tuple-element.15.direction_ref, ...), custom_call_target="tpu_custom_call" | custom-call | tf_op jit(solution)/shard_map/finish/pallas_call | solution.py:436
Async XLA Ops:
  0.6 18.7 %copy-start = (f32[48,2048]{1,0:T(8,128)S(1)}, f32[48,2048]{1,0:T(8,128)}, u32[]{:S(2)}) copy-start(f32[48,2048]{1,0:T(8,128)} %solution_ref.1) | copy-start | bytes 1179652
  0.6 18.7 %copy-start.1 = (s32[16]{0:T(128)S(1)}, s32[16]{0:T(128)}, u32[]{:S(2)}) copy-start(s32[16]{0:T(128)} %offsets_ref.1) | copy-start | bytes 196

commit v3 on v2

v3 whole, which is shorter than its diff:
```python
import functools

import jax
import jax.numpy as jnp
from jax import lax
from jax.experimental import pallas as pl
from jax.experimental.pallas import tpu as pltpu
from jax.sharding import PartitionSpec as P

LANES = 128
STATS = 5
PROJECT_MIB = 30
FINISH_MIB = 8


def split(value):
    upper = value.astype(jnp.bfloat16)
    return upper, (value - upper.astype(jnp.float32)).astype(jnp.bfloat16)


def fold_tile(value):
    total = None
    for r in range(0, value.shape[0], 8):
        for c in range(0, value.shape[1], LANES):
            tile = value[r : r + 8, c : c + LANES]
            total = tile if total is None else total + tile
    return total


def project(
    count,
    offsets_hbm,
    direction_hbm,
    gradient_hbm,
    residual_hbm,
    tiles_hbm,
    residual_vm,
    windows,
    direction_vm,
    back_image,
    back_residual,
    stats_out,
    offsets_sm,
    gradient_vm,
    tiles_vm,
    own,
    halo,
    images,
    hits,
    covers,
    covers_in,
    times,
    image_sums,
    sums_own,
    sums_out,
    sums_in,
    stacked,
    partial,
    stat_send,
    stat_recv,
    load_sems,
    residual_sems,
    tile_sems,
    side_send,
    cover_recv,
    sums_send,
    sums_recv,
    halo_recv,
    stat_sems,
):
    scope = jax.named_scope
    me = lax.axis_index("slab")
    planes, cells = direction_vm.shape
    per_angle, angles, rows, columns = residual_vm.shape
    near = 3 * planes
    half = angles // 2
    pairs = (range(0, half), range(half, angles))
    last = angles - 1
    f32, bf16 = jnp.float32, jnp.bfloat16
    has_low = me > 0
    has_high = me < count - 1
    late = me >= count - count // 4
    early = me < count // 2
    low = {"slab": lax.rem(me + count - 1, count)}
    high = {"slab": lax.rem(me + 1, count)}

    load_offsets = pltpu.make_async_copy(offsets_hbm, offsets_sm, load_sems.at[0])
    load_direction = pltpu.make_async_copy(direction_hbm, direction_vm, load_sems.at[1])
    load_gradient = pltpu.make_async_copy(gradient_hbm, gradient_vm, load_sems.at[0])

    groups = [(a, 1) for a in pairs[0]] + [(half, angles - half)]

    def load_residual(group):
        angles_of = pl.ds(*groups[group])
        return pltpu.make_async_copy(
            residual_hbm.at[:, angles_of], residual_vm.at[:, angles_of], residual_sems.at[group]
        )

    def load_tile(a):
        sem = residual_sems.at[0] if a == last else tile_sems.at[a]
        return pltpu.make_async_copy(tiles_hbm.at[a], tiles_vm.at[a], sem)

    load_offsets.start()
    for group in range(len(groups)):
        load_residual(group).start()
    load_direction.start()
    for a in range(last):
        load_tile(a).start(priority=1)

    barrier = pltpu.get_barrier_semaphore()
    for d in range(1, count):
        pl.semaphore_signal(barrier, inc=1, device_id={"slab": lax.rem(me + d, count)})

    @pl.when(jnp.logical_not(has_low))
    def _():
        halo[:planes, :] = jnp.zeros((planes, cells), bf16)
        covers_in[0] = jnp.zeros((planes, LANES), bf16)
        sums_in[0] = jnp.zeros((angles, planes, columns), bf16)

    @pl.when(jnp.logical_not(has_high))
    def _():
        halo[planes:, :] = jnp.zeros((planes, cells), bf16)
        covers_in[1] = jnp.zeros((planes, LANES), bf16)
        sums_in[1] = jnp.zeros((angles, planes, columns), bf16)

    with scope("w_off"):
        load_offsets.wait()
    shift = planes - me * planes

    lane = lax.broadcasted_iota(jnp.int32, (near, LANES), 1)
    plane = lax.broadcasted_iota(jnp.int32, (near, LANES), 0)
    first = jnp.full((near, LANES), near, jnp.int32)
    for v in range(angles * per_angle):
        first = jnp.where(lane == v, offsets_sm[v] + shift, first)
    inside = jnp.logical_and(plane >= first, plane < first + rows)
    covers[...] = jnp.where(inside, 1.0, 0.0).astype(bf16)

    plane_id = lax.broadcasted_iota(jnp.int32, (near, per_angle * rows), 0)
    row_id = lax.broadcasted_iota(jnp.int32, (near, per_angle * rows), 1)
    for a in range(angles):
        base = jnp.zeros_like(row_id)
        for j in range(per_angle):
            base = jnp.where(row_id >= j * rows, offsets_sm[j * angles + a] + shift - j * rows, base)
        hits[a] = jnp.where(plane_id == row_id + base, 1.0, 0.0).astype(bf16)

    def cover_copy(side):
        source = covers.at[pl.ds(0 if side == 0 else 2 * planes, planes)]
        return pltpu.make_async_remote_copy(
            source, covers_in.at[1 - side], side_send.at[side], cover_recv.at[1 - side],
            device_id=low if side == 0 else high,
        )

    def sums_copy(side, group):
        angles_of = pl.ds(*groups[group])
        return pltpu.make_async_remote_copy(
            sums_out.at[side, angles_of], sums_in.at[1 - side, angles_of],
            sums_send.at[side], sums_recv.at[1 - side, group // half],
            device_id=low if side == 0 else high,
        )

    def sums_wait(side, pair):
        landed = sums_in.at[side, pl.ds(pairs[pair][0], len(pairs[pair]))]
        pltpu.make_async_copy(landed, landed, sums_recv.at[side, pair]).wait()

    def sums_sent(side):
        pltpu.make_async_copy(sums_out.at[side], sums_out.at[side], sums_send.at[side]).wait()

    def halo_copy(side):
        return pltpu.make_async_remote_copy(
            own, halo.at[pl.ds((1 - side) * planes, planes)], side_send.at[side], halo_recv.at[1 - side],
            device_id=low if side == 0 else high,
        )

    def each_side(action):
        @pl.when(has_low)
        def _():
            action(0)

        @pl.when(has_high)
        def _():
            action(1)

    for group, (start, size) in enumerate(groups):
        with scope("w_res"):
            load_residual(group).wait()
        for a in range(start, start + size):
            upper, lower = split(residual_vm[:, a].reshape(per_angle * rows, columns))
            sums = jnp.dot(hits[a], upper, preferred_element_type=f32) + jnp.dot(
                hits[a], lower, preferred_element_type=f32
            )
            sums_own[a] = sums[planes : 2 * planes]
            sums_out[0, a] = sums[:planes].astype(bf16)
            sums_out[1, a] = sums[2 * planes :].astype(bf16)
        if group == 0:
            with scope("w_bar"):
                pl.semaphore_wait(barrier, count - 1)
            each_side(lambda side: cover_copy(side).start())
        each_side(lambda side: sums_copy(side, group).start())

    load_tile(last).start(priority=1)
    with scope("w_dir"):
        load_direction.wait()
    own[...] = direction_vm[...].astype(bf16)

    view_of = lax.broadcasted_iota(jnp.int32, (LANES, angles * LANES), 0)
    lane_of = lax.broadcasted_iota(jnp.int32, (LANES, angles * LANES), 1)
    chosen = jnp.where(lax.rem(view_of, angles) == lane_of // LANES, 1.0, 0.0).astype(bf16)
    product_sums = [jnp.zeros((8, LANES), f32)] * 3

    def backward(first_angle, last_angle):
        chunk = 2 * LANES
        for p in range(0, cells, chunk):
            part = None
            for a in range(first_angle, last_angle):
                product = lax.dot_general(
                    tiles_vm[a, p : p + chunk], stacked[a], (((1,), (1,)), ((), ())), preferred_element_type=f32
                )
                part = product if part is None else part + product
            if first_angle > 0:
                part = part + partial[p : p + chunk]
            if last_angle < angles:
                partial[p : p + chunk] = part
                continue
            turned = part.T
            from_image, from_residual = turned[:planes], turned[planes:]
            back_image[:, p : p + chunk] = from_image
            back_residual[:, p : p + chunk] = from_residual
            product_sums[0] = product_sums[0] + fold_tile(from_residual * from_residual)
            product_sums[1] = product_sums[1] + fold_tile(from_residual * from_image)
            product_sums[2] = product_sums[2] + fold_tile(from_image * from_image)

    def forward(a):
        image = jnp.dot(own[...], tiles_vm[a], preferred_element_type=f32)
        for l in range(columns // LANES):
            images[a, l, planes : 2 * planes] = image[:, l * LANES : (l + 1) * LANES]

    def count_covers():
        covered = covers[planes : 2 * planes].astype(f32) + covers_in[0].astype(f32) + covers_in[1].astype(f32)
        times[...] = jnp.dot(covered.astype(bf16), chosen, preferred_element_type=f32)

    def weigh(a):
        squares = None
        for l in range(columns // LANES):
            piece = images[a, l, planes : 2 * planes]
            weighted = times[:, a * LANES : (a + 1) * LANES] * piece
            stacked[a, :planes, l * LANES : (l + 1) * LANES] = weighted.astype(bf16)
            square = fold_tile(weighted * piece)
            squares = square if squares is None else squares + square
        image_sums[a] = squares

    def wait_tile(a):
        with scope("w_tile"):
            load_tile(a).wait()

    for a in pairs[0]:
        wait_tile(a)
        forward(a)
    with scope("w_cov"):
        each_side(lambda side: cover_copy(side).wait_send())
        each_side(lambda side: cover_copy(1 - side).wait_recv())
    each_side(lambda side: halo_copy(side).start())

    @pl.when(jnp.logical_not(late))
    def _():
        for a in range(half, last):
            wait_tile(a)
            if a == half:
                count_covers()
                weigh(0)
            forward(a)
        for a in range(1, last):
            weigh(a)

    @pl.when(early)
    def _():
        wait_tile(last)
        forward(last)
        weigh(last)

    @pl.when(late)
    def _():
        count_covers()
        for a in pairs[0]:
            weigh(a)

    def stack(pair):
        with scope("w_sums"):
            each_side(lambda side: sums_wait(side, pair))
        for a in pairs[pair]:
            sums = sums_own[a] + sums_in[0, a].astype(f32) + sums_in[1, a].astype(f32)
            stacked[a, planes:] = sums.astype(bf16)

    stack(0)
    load_gradient.start(priority=1)
    with scope("bwd"):
        backward(0, half)

    @pl.when(late)
    def _():
        for a in pairs[1]:
            wait_tile(a)
        for a in pairs[1]:
            forward(a)
        for a in pairs[1]:
            weigh(a)

    @pl.when(jnp.logical_not(jnp.logical_or(early, late)))
    def _():
        wait_tile(last)
        forward(last)
        weigh(last)

    with scope("w_grad"):
        load_gradient.wait()
    stack(1)
    with scope("bwd"):
        gradient_sums = fold_tile(gradient_vm[...] * gradient_vm[...])
        backward(half, angles)

    image_total = image_sums[0]
    for a in range(1, angles):
        image_total = image_total + image_sums[a]
    stat_send[...] = jnp.concatenate(
        [jnp.sum(x, axis=0, keepdims=True) for x in [gradient_sums, image_total] + product_sums]
        + [jnp.zeros((8 - STATS, LANES), f32)],
        axis=0,
    )
    for d in range(1, count):
        pltpu.make_async_remote_copy(
            stat_send, stat_recv.at[d - 1], stat_sems.at[0], stat_sems.at[1],
            device_id={"slab": lax.rem(me + d, count)},
        ).start()

    with scope("w_halo"):
        each_side(lambda side: halo_copy(side).wait_send())
        each_side(lambda side: halo_copy(1 - side).wait_recv())

    with scope("fwdhalo"):
        for a in range(angles):
            image = jnp.dot(halo[...], tiles_vm[a], preferred_element_type=f32)
            for l in range(columns // LANES):
                cut = slice(l * LANES, (l + 1) * LANES)
                images[a, l, :planes] = image[:planes, cut]
                images[a, l, 2 * planes :] = image[planes:, cut]

    with scope("windows"):
        for j in range(per_angle):
            for a in range(angles):
                top = jnp.clip(offsets_sm[j * angles + a] + shift, 0, near - rows)
                for l in range(columns // LANES):
                    windows[j, a, :, l * LANES : (l + 1) * LANES] = images[a, l, pl.ds(top, rows), :]

    each_side(sums_sent)
    with scope("w_stat"):
        pltpu.make_async_copy(stat_recv, stat_recv, stat_sems.at[0]).wait()
        pltpu.make_async_copy(stat_recv, stat_recv, stat_sems.at[1]).wait()
    sums = stat_send[...]
    for d in range(1, count):
        sums = sums + stat_recv[d - 1]
    norms = jnp.sum(sums, axis=1, keepdims=True)
    grad_norm, image_norm = norms[0:1], norms[1:2]
    step_size = grad_norm / image_norm
    new_norm = norms[2:3] - 2.0 * step_size * norms[3:4] + step_size * step_size * norms[4:5]
    stats_out[...] = jnp.concatenate(
        [
            jnp.broadcast_to(step_size, (1, LANES)),
            jnp.broadcast_to(new_norm / grad_norm, (1, LANES)),
            jnp.zeros((6, LANES), f32),
        ],
        axis=0,
    )


def finish(
    stats, solution_ref, direction_ref, back_image, back_residual, windows, residual_ref,
    solution_out, residual_out, gradient_out, direction_out,
    volumes_vm, residual_vm, sems,
):
    per_angle, angles = residual_ref.shape[:2]
    step_size = stats[0:1, 0:1]
    scale = stats[1:2, 0:1]
    for j in range(per_angle):
        for a in range(angles):
            residual_vm[j, a] = residual_ref[j, a] - step_size * windows[j, a]
            pltpu.make_async_copy(residual_vm.at[j, a], residual_out.at[j, a], sems.at[0]).start()
    gradient = back_residual[...] - step_size * back_image[...]
    volumes_vm[0] = gradient
    pltpu.make_async_copy(volumes_vm.at[0], gradient_out, sems.at[1]).start()
    volumes_vm[1] = gradient + scale * direction_ref[...]
    pltpu.make_async_copy(volumes_vm.at[1], direction_out, sems.at[1]).start()
    volumes_vm[2] = solution_ref[...] + step_size * direction_ref[...]
    pltpu.make_async_copy(volumes_vm.at[2], solution_out, sems.at[1]).start()
    pltpu.make_async_copy(residual_vm, residual_out, sems.at[0]).wait()
    pltpu.make_async_copy(volumes_vm, volumes_vm, sems.at[1]).wait()


def local(count, solution, direction, gradient, residual, tiles, offsets):
    planes, cells = solution.shape
    views, rows, columns = residual.shape
    angles = tiles.shape[0]
    per_angle = views // angles
    near = 3 * planes
    half = angles // 2
    f32, bf16 = jnp.float32, jnp.bfloat16
    hbm = pl.BlockSpec(memory_space=pltpu.HBM)
    vmem = pl.BlockSpec(memory_space=pltpu.VMEM)
    dma = pltpu.SemaphoreType.DMA
    by_angle = residual.reshape(per_angle, angles, rows, columns)
    volume = jax.ShapeDtypeStruct((planes, cells), f32)
    detector = jax.ShapeDtypeStruct(by_angle.shape, f32)
    remote = [pltpu.with_memory_space_constraint(x, pltpu.HBM) for x in (offsets, direction, gradient, by_angle, tiles)]
    residual_in, windows, direction_in, back_image, back_residual, stats = pl.pallas_call(
        functools.partial(project, count),
        name="project",
        out_shape=(detector, detector, volume, volume, volume, jax.ShapeDtypeStruct((8, LANES), f32)),
        in_specs=[hbm] * 5,
        out_specs=(vmem,) * 6,
        scratch_shapes=[
            pltpu.SMEM((views,), jnp.int32),
            pltpu.VMEM((planes, cells), f32),
            pltpu.VMEM((angles, cells, columns), bf16),
            pltpu.VMEM((planes, cells), bf16),
            pltpu.VMEM((2 * planes, cells), bf16),
            pltpu.VMEM((angles, columns // LANES, near, LANES), f32),
            pltpu.VMEM((angles, near, per_angle * rows), bf16),
            pltpu.VMEM((near, LANES), bf16),
            pltpu.VMEM((2, planes, LANES), bf16),
            pltpu.VMEM((planes, angles * LANES), f32),
            pltpu.VMEM((angles, 8, LANES), f32),
            pltpu.VMEM((angles, planes, columns), f32),
            pltpu.VMEM((2, angles, planes, columns), bf16),
            pltpu.VMEM((2, angles, planes, columns), bf16),
            pltpu.VMEM((angles, 2 * planes, columns), bf16),
            pltpu.VMEM((cells, 2 * planes), f32),
            pltpu.VMEM((8, LANES), f32),
            pltpu.VMEM((count - 1, 8, LANES), f32),
            dma((2,)),
            dma((half + 1,)),
            dma((angles - 1,)),
            dma((2,)),
            dma((2,)),
            dma((2,)),
            dma((2, 2)),
            dma((2,)),
            dma((2,)),
        ],
        compiler_params=pltpu.CompilerParams(
            collective_id=0, has_side_effects=True, vmem_limit_bytes=PROJECT_MIB * 1024 * 1024
        ),
    )(*remote)
    results = pl.pallas_call(
        finish,
        name="finish",
        out_shape=(volume, detector, volume, volume),
        in_specs=[vmem] * 7,
        out_specs=(hbm,) * 4,
        scratch_shapes=[
            pltpu.VMEM((3, planes, cells), f32),
            pltpu.VMEM(by_angle.shape, f32),
            dma((2,)),
        ],
        compiler_params=pltpu.CompilerParams(vmem_limit_bytes=FINISH_MIB * 1024 * 1024),
    )(stats, solution, direction_in, back_image, back_residual, windows, residual_in)
    return results[0], results[1].reshape(residual.shape), results[2], results[3]


def solution(mesh):
    placed = (
        P(("scan", "slab"), None),
        P(("scan", "slab"), None),
        P(("scan", "slab"), None),
        P(("scan", "slab"), None, None),
        P(),
        P(("scan", "slab")),
    )
    return jax.shard_map(
        functools.partial(local, mesh.shape["slab"]),
        mesh=mesh,
        in_specs=placed,
        out_specs=(
            P(("scan", "slab"), None),
            P(("scan", "slab"), None, None),
            P(("scan", "slab"), None),
            P(("scan", "slab"), None),
        ),
        check_vma=False,
    )
```

time: 22.5 us -> 21.1 us (0.938)
  Pallas kernels: 21.7 us -> 20.3 us
    pallas_call x1, Pallas kernels: 18.7 us -> 18 us  [local(): pl.pallas_call(functools.partial(project, count), name='project', out_sha...]
    pallas_call x1, Pallas kernels: 2.96 us -> 2.29 us  [local(): pl.pallas_call(finish, name='finish', out_shape=(volume, detector, volume...]
where the time goes in v3:
time: 21.1 us; the launch traced here: 20.9 us
  Pallas kernels  20.3 us (96%)
  between operations  0.66 us (3%)
    pallas_call x1, Pallas kernels, local(): pl.pallas_call(functools.partial(project, count), name='project', out_sha...  18 us
    pallas_call x1, Pallas kernels, local(): pl.pallas_call(finish, name='finish', out_shape=(volume, detector, volume...  2.29 us

profile of v3, /device:TPU:0, one launch (start us, length us, event | category | flops | bytes accessed | tf_op | source)
XLA Modules:
  0.0 20.9 jit_solution(10054156959706791695)
XLA Ops:
  0.6 0.0 copy-start
  0.6 18.0 %project.1 = (f32[4,4,64,896]{3,2,1,0:T(8,128)S(1)}, f32[4,4,64,896]{3,2,1,0:T(8,128)S(1)}, f32[48,2048]{1,0:T(8,128)S(1)}, f32[48,2048]{1,0:T(8,128)S(1)}, f32[...) custom-call(s32[16]{0:T(128)} %offsets_hbm.1, f32[48,2048]{1,0:T(8,128)} %direction_hbm.1, f32[48,2048]{1,0:T(8,128)} %gradient_hbm.1, ...), custom_call_target="tpu_custom_call" | custom-call | tf_op jit(solution)/shard_map/project/pallas_call | solution.py:412
  18.6 0.0 copy-done
  18.6 2.3 %finish.1 = (f32[48,2048]{1,0:T(8,128)}, f32[4,4,64,896]{3,2,1,0:T(8,128)}, f32[48,2048]{1,0:T(8,128)}, f32[48,2048]{1,0:T(8,128)}) custom-call(f32[8,128]{1,0:T(8,128)S(1)} %get-tuple-element.14.stats, f32[48,2048]{1,0:T(8,128)S(1)} %copy-done, f32[48,2048]{1,0:T(8,128)S(1)} %get-tuple-element.15.direction_ref, ...), custom_call_target="tpu_custom_call" | custom-call | tf_op jit(solution)/shard_map/finish/pallas_call | solution.py:451
Async XLA Ops:
  0.6 18.0 %copy-start = (f32[48,2048]{1,0:T(8,128)S(1)}, f32[48,2048]{1,0:T(8,128)}, u32[]{:S(2)}) copy-start(f32[48,2048]{1,0:T(8,128)} %solution_ref.1) | copy-start | bytes 1179652

commit v4 on v3

--- a/solution.py
+++ b/solution.py
@@ -51,6 +51,8 @@
     covers_in,
     times,
     image_sums,
+    product_sums,
+    gradient_sums,
     sums_own,
     sums_out,
     sums_in,
@@ -96,16 +98,21 @@
             residual_hbm.at[:, angles_of], residual_vm.at[:, angles_of], residual_sems.at[group]
         )
 
-    def load_tile(a):
-        sem = residual_sems.at[0] if a == last else tile_sems.at[a]
-        return pltpu.make_async_copy(tiles_hbm.at[a], tiles_vm.at[a], sem)
+    middle = cells // 2
+    pieces = {a: ((0, cells),) if a in (0, last) else ((0, middle), (middle, cells - middle)) for a in range(angles)}
+
+    def load_tile(a, part):
+        cut = pl.ds(*pieces[a][part])
+        sem = residual_sems.at[0] if a == last else tile_sems.at[2 * a + part]
+        return pltpu.make_async_copy(tiles_hbm.at[a, cut], tiles_vm.at[a, cut], sem)
 
     load_offsets.start()
     for group in range(len(groups)):
         load_residual(group).start()
     load_direction.start()
     for a in range(last):
-        load_tile(a).start(priority=1)
+        for part in range(len(pieces[a])):
+            load_tile(a, part).start(priority=1)
 
     barrier = pltpu.get_barrier_semaphore()
     for d in range(1, count):
@@ -154,13 +161,9 @@
         angles_of = pl.ds(*groups[group])
         return pltpu.make_async_remote_copy(
             sums_out.at[side, angles_of], sums_in.at[1 - side, angles_of],
-            sums_send.at[side], sums_recv.at[1 - side, group // half],
+            sums_send.at[side], sums_recv.at[1 - side, group],
             device_id=low if side == 0 else high,
         )
-
-    def sums_wait(side, pair):
-        landed = sums_in.at[side, pl.ds(pairs[pair][0], len(pairs[pair]))]
-        pltpu.make_async_copy(landed, landed, sums_recv.at[side, pair]).wait()
 
     def sums_sent(side):
         pltpu.make_async_copy(sums_out.at[side], sums_out.at[side], sums_send.at[side]).wait()
@@ -183,6 +186,8 @@
     for group, (start, size) in enumerate(groups):
         with scope("w_res"):
             load_residual(group).wait()
+        if group == 0:
+            load_tile(last, 0).start(priority=1)
         for a in range(start, start + size):
             upper, lower = split(residual_vm[:, a].reshape(per_angle * rows, columns))
             sums = jnp.dot(hits[a], upper, preferred_element_type=f32) + jnp.dot(
@@ -197,7 +202,6 @@
             each_side(lambda side: cover_copy(side).start())
         each_side(lambda side: sums_copy(side, group).start())
 
-    load_tile(last).start(priority=1)
     with scope("w_dir"):
         load_direction.wait()
     own[...] = direction_vm[...].astype(bf16)
@@ -205,10 +209,10 @@
     view_of = lax.broadcasted_iota(jnp.int32, (LANES, angles * LANES), 0)
     lane_of = lax.broadcasted_iota(jnp.int32, (LANES, angles * LANES), 1)
     chosen = jnp.where(lax.rem(view_of, angles) == lane_of // LANES, 1.0, 0.0).astype(bf16)
-    product_sums = [jnp.zeros((8, LANES), f32)] * 3
 
     def backward(first_angle, last_angle):
         chunk = 2 * LANES
+        squares = [None] * 3
         for p in range(0, cells, chunk):
             part = None
             for a in range(first_angle, last_angle):
@@ -225,14 +229,21 @@
             from_image, from_residual = turned[:planes], turned[planes:]
             back_image[:, p : p + chunk] = from_image
             back_residual[:, p : p + chunk] = from_residual
-            product_sums[0] = product_sums[0] + fold_tile(from_residual * from_residual)
-            product_sums[1] = product_sums[1] + fold_tile(from_residual * from_image)
-            product_sums[2] = product_sums[2] + fold_tile(from_image * from_image)
-
-    def forward(a):
-        image = jnp.dot(own[...], tiles_vm[a], preferred_element_type=f32)
+            for k, (x, y) in enumerate(((from_residual, from_residual), (from_residual, from_image), (from_image, from_image))):
+                square = fold_tile(x * y)
+                squares[k] = square if squares[k] is None else squares[k] + square
+        if last_angle == angles:
+            for k in range(3):
+                product_sums[k] = squares[k]
+
+    def forward(a, start=0, size=cells):
+        cut = pl.ds(start, size)
+        image = jnp.dot(own[:, cut], tiles_vm[a, cut], preferred_element_type=f32)
         for l in range(columns // LANES):
-            images[a, l, planes : 2 * planes] = image[:, l * LANES : (l + 1) * LANES]
+            piece = image[:, l * LANES : (l + 1) * LANES]
+            if start > 0:
+                piece = piece + images[a, l, planes : 2 * planes]
+            images[a, l, planes : 2 * planes] = piece
 
     def count_covers():
         covered = covers[planes : 2 * planes].astype(f32) + covers_in[0].astype(f32) + covers_in[1].astype(f32)
@@ -248,88 +259,112 @@
             squares = square if squares is None else squares + square
         image_sums[a] = squares
 
+    def wait_part(a, part):
+        with scope("w_tile"):
+            load_tile(a, part).wait()
+
     def wait_tile(a):
-        with scope("w_tile"):
-            load_tile(a).wait()
-
-    for a in pairs[0]:
-        wait_tile(a)
-        forward(a)
-    with scope("w_cov"):
-        each_side(lambda side: cover_copy(side).wait_send())
-        each_side(lambda side: cover_copy(1 - side).wait_recv())
-    each_side(lambda side: halo_copy(side).start())
-
-    @pl.when(jnp.logical_not(late))
-    def _():
-        for a in range(half, last):
-            wait_tile(a)
-            if a == half:
-                count_covers()
-                weigh(0)
-            forward(a)
-        for a in range(1, last):
-            weigh(a)
-
-    @pl.when(early)
-    def _():
-        wait_tile(last)
-        forward(last)
-        weigh(last)
-
-    @pl.when(late)
-    def _():
+        for part in range(len(pieces[a])):
+            wait_part(a, part)
+
+    def forward_parts(a, before=()):
+        for part, (start, size) in enumerate(pieces[a]):
+            wait_part(a, part)
+            if part == 0:
+                for action in before:
+                    action()
+            forward(a, start, size)
+
+    def take_covers():
+        with scope("w_cov"):
+            each_side(lambda side: cover_copy(side).wait_send())
+            each_side(lambda side: cover_copy(1 - side).wait_recv())
+        each_side(lambda side: halo_copy(side).start())
+
+    def wait_sums(start, stop):
+        for group, (first_angle, size) in enumerate(groups):
+            if start <= first_angle < stop:
+                with scope("w_sums"):
+                    each_side(lambda side: sums_copy(1 - side, group).wait_recv())
+
+    def stack(start, stop):
+        for a in range(start, stop):
+            sums = sums_own[a] + sums_in[0, a].astype(f32) + sums_in[1, a].astype(f32)
+            stacked[a, planes:] = sums.astype(bf16)
+
+    def weigh_first():
         count_covers()
         for a in pairs[0]:
             weigh(a)
 
-    def stack(pair):
-        with scope("w_sums"):
-            each_side(lambda side: sums_wait(side, pair))
-        for a in pairs[pair]:
-            sums = sums_own[a] + sums_in[0, a].astype(f32) + sums_in[1, a].astype(f32)
-            stacked[a, planes:] = sums.astype(bf16)
-
-    stack(0)
-    load_gradient.start(priority=1)
-    with scope("bwd"):
-        backward(0, half)
+    def first_pair():
+        wait_sums(0, half)
+        load_gradient.start(priority=1)
+        with scope("bwd"):
+            stack(0, half)
+            backward(0, half)
+
+    def second_pair(angles_left):
+        for a in angles_left:
+            wait_tile(a)
+        with scope("w_grad"):
+            load_gradient.wait()
+        wait_sums(half, angles)
+        with scope("bwd2"):
+            gradient_sums[...] = fold_tile(gradient_vm[...] * gradient_vm[...])
+            stack(half, angles)
+            for a in angles_left:
+                forward(a)
+            for a in angles_left:
+                weigh(a)
+            backward(half, angles)
+            image_total = image_sums[0]
+            for a in range(1, angles):
+                image_total = image_total + image_sums[a]
+            parts = (gradient_sums[...], image_total, product_sums[0], product_sums[1], product_sums[2])
+            stat_send[...] = jnp.concatenate([jnp.sum(x, axis=0, keepdims=True) for x in parts], axis=0)
+        for d in range(1, count):
+            pltpu.make_async_remote_copy(
+                stat_send, stat_recv.at[d - 1], stat_sems.at[0], stat_sems.at[1],
+                device_id={"slab": lax.rem(me + d, count)},
+            ).start()
 
     @pl.when(late)
     def _():
-        for a in pairs[1]:
-            wait_tile(a)
-        for a in pairs[1]:
-            forward(a)
-        for a in pairs[1]:
+        wait_tile(0)
+        forward(0)
+        take_covers()
+        for a in range(1, half):
+            forward_parts(a, (count_covers, functools.partial(weigh, 0)) if a == 1 else ())
             weigh(a)
+        first_pair()
+        second_pair(range(half, angles))
 
     @pl.when(jnp.logical_not(jnp.logical_or(early, late)))
     def _():
-        wait_tile(last)
-        forward(last)
-        weigh(last)
-
-    with scope("w_grad"):
-        load_gradient.wait()
-    stack(1)
-    with scope("bwd"):
-        gradient_sums = fold_tile(gradient_vm[...] * gradient_vm[...])
-        backward(half, angles)
-
-    image_total = image_sums[0]
-    for a in range(1, angles):
-        image_total = image_total + image_sums[a]
-    stat_send[...] = jnp.concatenate(
-        [jnp.sum(x, axis=0, keepdims=True) for x in [gradient_sums, image_total] + product_sums]
-        + [jnp.zeros((8 - STATS, LANES), f32)],
-        axis=0,
-    )
-    for d in range(1, count):
-        pltpu.make_async_remote_copy(
-            stat_send, stat_recv.at[d - 1], stat_sems.at[0], stat_sems.at[1],
-            device_id={"slab": lax.rem(me + d, count)},
-        ).start()
+        for a in pairs[0]:
+            forward_parts(a)
+        take_covers()
+        for a in range(half, last):
+            forward_parts(a, (weigh_first,) if a == half else ())
+            weigh(a)
+        first_pair()
+        second_pair(range(last, angles))
+
+    @pl.when(early)
+    def _():
+        for a in pairs[0]:
+            wait_tile(a)
+            forward(a)
+        take_covers()
+        for a in range(half, angles):
+            wait_tile(a)
+            if a == half:
+                weigh_first()
+            forward(a)
+            weigh(a)
+        first_pair()
+        second_pair(())
 
     with scope("w_halo"):
         each_side(lambda side: halo_copy(side).wait_send())
@@ -427,20 +462,22 @@
             pltpu.VMEM((2, planes, LANES), bf16),
             pltpu.VMEM((planes, angles * LANES), f32),
             pltpu.VMEM((angles, 8, LANES), f32),
+            pltpu.VMEM((3, 8, LANES), f32),
+            pltpu.VMEM((8, LANES), f32),
             pltpu.VMEM((angles, planes, columns), f32),
             pltpu.VMEM((2, angles, planes, columns), bf16),
             pltpu.VMEM((2, angles, planes, columns), bf16),
             pltpu.VMEM((angles, 2 * planes, columns), bf16),
             pltpu.VMEM((cells, 2 * planes), f32),
-            pltpu.VMEM((8, LANES), f32),
-            pltpu.VMEM((count - 1, 8, LANES), f32),
+            pltpu.VMEM((STATS, LANES), f32),
+            pltpu.VMEM((count - 1, STATS, LANES), f32),
             dma((2,)),
             dma((half + 1,)),
-            dma((angles - 1,)),
-            dma((2,)),
-            dma((2,)),
-            dma((2,)),
-            dma((2, 2)),
+            dma((2 * angles - 2,)),
+            dma((2,)),
+            dma((2,)),
+            dma((2,)),
+            dma((2, half + 1)),
             dma((2,)),
             dma((2,)),
         ],

time: 21.1 us -> 20.9 us (level)
  Pallas kernels: 20.3 us -> 20 us
    pallas_call x1, Pallas kernels: 18 us -> 17.7 us  [local(): pl.pallas_call(functools.partial(project, count), name='project', out_sha...]
where the time goes in v4:
time: 20.9 us; the launch traced here: 20.8 us
  Pallas kernels  20 us (96%)
  between operations  0.84 us (4%)
    pallas_call x1, Pallas kernels, local(): pl.pallas_call(functools.partial(project, count), name='project', out_sha...  17.7 us
    pallas_call x1, Pallas kernels, local(): pl.pallas_call(finish, name='finish', out_shape=(volume, detector, volume...  2.29 us

profile of v4, /device:TPU:0, one launch (start us, length us, event | category | flops | bytes accessed | tf_op | source)
XLA Modules:
  0.0 20.8 jit_solution(8615071956716082799)
XLA Ops:
  0.6 0.0 copy-start
  0.6 17.7 %project.1 = (f32[4,4,64,896]{3,2,1,0:T(8,128)S(1)}, f32[4,4,64,896]{3,2,1,0:T(8,128)S(1)}, f32[48,2048]{1,0:T(8,128)S(1)}, f32[48,2048]{1,0:T(8,128)S(1)}, f32[...) custom-call(s32[16]{0:T(128)} %offsets_hbm.1, f32[48,2048]{1,0:T(8,128)} %direction_hbm.1, f32[48,2048]{1,0:T(8,128)} %gradient_hbm.1, ...), custom_call_target="tpu_custom_call" | custom-call | tf_op jit(solution)/shard_map/project/pallas_call | solution.py:447
  18.3 0.0 copy-done
  18.3 2.3 %finish.1 = (f32[48,2048]{1,0:T(8,128)}, f32[4,4,64,896]{3,2,1,0:T(8,128)}, f32[48,2048]{1,0:T(8,128)}, f32[48,2048]{1,0:T(8,128)}) custom-call(f32[8,128]{1,0:T(8,128)S(1)} %get-tuple-element.14.stats, f32[48,2048]{1,0:T(8,128)S(1)} %copy-done, f32[48,2048]{1,0:T(8,128)S(1)} %get-tuple-element.15.direction_ref, ...), custom_call_target="tpu_custom_call" | custom-call | tf_op jit(solution)/shard_map/finish/pallas_call | solution.py:488
Async XLA Ops:
  0.6 17.7 %copy-start = (f32[48,2048]{1,0:T(8,128)S(1)}, f32[48,2048]{1,0:T(8,128)}, u32[]{:S(2)}) copy-start(f32[48,2048]{1,0:T(8,128)} %solution_ref.1) | copy-start | bytes 1179652
